TPU v7x, 32 devices: a whole 2x2x4 slice. The times are simulated.
32 devices in a mesh: expert: 16 (over z, y, x), replica: 2 (over core).
Axes of the slice: x: 2, y: 2, z: 4, core: 2. Of those that a mesh axis runs over, the one named last changes fastest.
Arguments:
- tokens: bfloat16 [16384, 1024], P(('expert', 'replica')), may hold values from -6 to 6
- expert_id: int32 [16384, 1], P(('expert', 'replica')), may hold values from 0 to 15; in each aligned block of 512 rows (0 to 511, 512 to 1023, ...) at most 64 rows name the same one
- router_prob: float32 [16384], P(('expert', 'replica')), may hold values from 0.1 to 1
- keep_mask: int32 [16, 32, 2048], P('expert'), may hold values 0 or 1
- w_in: bfloat16 [16, 1024, 2048], P('expert'), may hold values from -0.1875 to 0.1875
- w_out: bfloat16 [16, 2048, 1024], P('expert'), may hold values from -0.125 to 0.125
- cotangent: bfloat16 [16384, 1024], P(('expert', 'replica')), may hold values from -0.59765625 to 0.59765625
Outputs:
- mixed: bfloat16 [16384, 1024], P(('expert', 'replica'))
- grad_in: float32 [16, 1024, 2048], P('expert', 'replica')
- grad_out: float32 [16, 2048, 1024], P('expert', 'replica')
Inputs may be any that keep to these rules, and one draw needn't show every extreme that they name: `expert_id`: among the 512 tokens of one device no expert is chosen more than 64 times; on some devices one expert is chosen exactly 64 times.
All inputs are finite; a program needn't handle non-finite values. No bound on the sum of `keep_mask` on one device may be relied on, other than what follows from the above.
Results may differ from a plain program's by a relative error of at most 0.0057.
Values may be sent and summed in bfloat16 or wider, within the bound.
A program may use at most 128 MiB of HBM per device.

v0:
```python
import jax
import jax.numpy as jnp
from jax import lax
from jax.sharding import PartitionSpec as P

KEEP_SCALE = 4.0 / 3.0


def gelu_parts(pre):
    inner = 0.7978845608 * (pre + 0.044715 * pre * pre * pre)
    tanh_v = jnp.tanh(inner)
    value = 0.5 * pre * (1.0 + tanh_v)
    slope = 0.5 * (1.0 + tanh_v) + 0.5 * pre * (1.0 - tanh_v * tanh_v) * 0.7978845608 * (
        1.0 + 3.0 * 0.044715 * pre * pre
    )
    return (value, slope)


def hidden_parts(received, keep_scale, weight_in):
    sources, slots, width = received.shape
    pre = jnp.dot(
        received.reshape(sources * slots, width), weight_in, preferred_element_type=jnp.float32
    )
    value, slope = gelu_parts(pre)
    value = value.reshape(sources, slots, -1)
    hidden = (value * keep_scale[:, None, :]).astype(jnp.bfloat16)
    return (hidden, slope.reshape(sources, slots, -1))


def expert_forward(received, keep_scale, weight_in, weight_out):
    sources, slots, width = received.shape
    hidden, slope = hidden_parts(received, keep_scale, weight_in)
    out = jnp.dot(
        hidden.reshape(sources * slots, -1), weight_out, preferred_element_type=jnp.float32
    )
    return (out.astype(jnp.bfloat16).reshape(sources, slots, width), hidden, slope)


def copies_backward(received, grad_rows, hidden, slope, keep_scale, weight_out):
    sources, slots, width = received.shape
    hidden_width = weight_out.shape[0]
    rows_x = received.reshape(sources * slots, width)
    rows_g = grad_rows.reshape(sources * slots, width)
    flat_hidden = hidden.reshape(sources * slots, hidden_width)
    dhidden = lax.dot_general(
        rows_g, weight_out, (((1,), (1,)), ((), ())), preferred_element_type=jnp.float32
    )
    dpre = (dhidden.reshape(sources, slots, hidden_width) * keep_scale[:, None, :] * slope).astype(
        jnp.bfloat16
    )
    dpre = dpre.reshape(sources * slots, hidden_width)
    columns = flat_hidden
    grad_out = lax.psum_scatter(
        lax.dot_general(
            columns, rows_g, (((0,), (0,)), ((), ())), preferred_element_type=jnp.float32
        ),
        "replica",
        scatter_dimension=0,
        tiled=True,
    )
    columns = rows_x
    grad_in = lax.psum_scatter(
        lax.dot_general(
            columns, dpre, (((0,), (0,)), ((), ())), preferred_element_type=jnp.float32
        ),
        "replica",
        scatter_dimension=0,
        tiled=True,
    )
    return (grad_in, grad_out)


def shards(tokens, expert_id, router_prob, keep_mask, w_in, w_out, cotangent):
    tok_rows, width = tokens.shape
    n_expert = lax.axis_size("expert")
    n_replica = lax.axis_size("replica")
    capacity = 2 * tok_rows // n_expert
    portion = capacity // n_replica
    weight_in = w_in[0]
    weight_out = w_out[0]
    ids = expert_id[:, 0]
    onehot = (ids[:, None] == jnp.arange(n_expert, dtype=jnp.int32)[None, :]).astype(jnp.int32)
    ranks = jnp.sum(jnp.cumsum(onehot, axis=0) * onehot, axis=1) - 1
    target = ids * capacity + ranks % n_replica * portion + ranks // n_replica

    def fill_slots(values):
        return jnp.zeros((n_expert * capacity, width), values.dtype).at[target].set(values)

    sent = fill_slots(tokens)
    gated = (router_prob[:, None] * cotangent.astype(jnp.float32)).astype(jnp.bfloat16)
    sent_grad = fill_slots(gated)
    keep_rows = lax.dynamic_index_in_dim(
        keep_mask[0].reshape(n_expert, n_replica, -1),
        lax.axis_index("replica"),
        axis=1,
        keepdims=False,
    )
    keep_scale = keep_rows.astype(jnp.float32) * KEEP_SCALE
    received = lax.all_to_all(
        sent.reshape(n_expert, capacity, width), "expert", split_axis=0, concat_axis=0, tiled=True
    )
    out, hidden, slope = expert_forward(received, keep_scale, weight_in, weight_out)
    back = lax.all_to_all(out, "expert", split_axis=0, concat_axis=0, tiled=True)
    results = (back, received, hidden, slope)
    grad_rows = lax.all_to_all(
        sent_grad.reshape(n_expert, capacity, width),
        "expert",
        split_axis=0,
        concat_axis=0,
        tiled=True,
    )
    returned = results[0]
    received = results[1]
    hidden, slope = (results[2], results[3])
    grad_in, grad_out = copies_backward(received, grad_rows, hidden, slope, keep_scale, weight_out)
    expert_out = returned.reshape(n_expert * capacity, width)[target]
    mixed = (router_prob[:, None] * expert_out.astype(jnp.float32)).astype(jnp.bfloat16)
    return (mixed, grad_in[None], grad_out[None])


def solution(mesh):
    in_specs = (
        P(("expert", "replica"), None),
        P(("expert", "replica"), None),
        P(("expert", "replica")),
        P("expert", None, None),
        P("expert", None, None),
        P("expert", None, None),
        P(("expert", "replica"), None),
    )
    out_specs = (
        P(("expert", "replica"), None),
        P("expert", "replica", None),
        P("expert", "replica", None),
    )
    return jax.shard_map(shards, mesh=mesh, in_specs=in_specs, out_specs=out_specs, check_vma=False)
```

profile of v0, /device:TPU:0, one launch (start us, length us, event | category | flops | bytes accessed | tf_op | source)
XLA Modules:
  0.0 220.8 jit_solution(9866834773011733649)
XLA Ops:
  7.2 0.0 copy-start.2
  7.2 0.0 copy-start
  7.2 0.8 fusion.24
  8.0 1.1 reduce-window.6
  9.1 0.2 slice_reduce_fusion
  9.4 0.8 fusion.23
  10.1 0.7 compare_select_fusion
  10.9 4.8 %scatter_custom_fusion = bf16[1024,1024]{1,0:T(8,128)(2,1)} fusion(s32[512]{0:T(512)S(1)} %bitcast.69, bf16[512,1024]{1,0:T(8,128)(2,1)} %param.7, bf16[]{:T(256)} %constant.29.clone.1), kind=kCustom, calls=%fused_computation.28 | custom fusion | bytes 2097664 | tf_op jit(solution)/shard_map/scatter | solution.py:87
  15.6 8.3 %all-to-all-start = ((bf16[16,64,1024]{2,1,0:T(8,128)(2,1)}), bf16[16,64,1024]{2,1,0:T(8,128)(2,1)S(1)}, u32[]{:S(2)}, u32[]{:S(2)}) async-start(bf16[16,64,1024]{2,1,0:T(8,128)(2,1)} %bitcast.5), calls=%async_computation | async-start | bytes 4194304 | tf_op jit(solution)/shard_map/all_to_all | solution.py:99
  24.0 0.0 copy-done.2
  24.0 0.0 copy-done
  24.0 0.0 copy-start.1
  24.0 4.2 %scatter_custom_fusion.1 = bf16[1024,1024]{1,0:T(8,128)(2,1)} fusion(s32[512]{0:T(512)S(1)} %bitcast.70, bf16[512,1024]{1,0:T(8,128)(2,1)S(1)} %copy-done, bf16[]{:T(256)} %constant.29.clone.1, f32[512]{0:T(512)S(1)} %copy-done.2), kind=kCustom, calls=%fused_computation.26 | custom fusion | flops 1572864 | bytes 3147778 | tf_op jit(solution)/shard_map/scatter | solution.py:87
  28.2 38.8 %all-to-all-done = bf16[16,64,1024]{2,1,0:T(8,128)(2,1)S(1)} async-done(((bf16[16,64,1024]{2,1,0:T(8,128)(2,1)}), bf16[16,64,1024]{2,1,0:T(8,128)(2,1)S(1)}, u32[]{:S(2)}, u32[]{:S(2)}) %all-to-all-start) | async-done | bytes 2097184 | tf_op jit(solution)/shard_map/all_to_all | solution.py:99
  67.0 10.1 %all-to-all-start.2 = ((bf16[16,64,1024]{2,1,0:T(8,128)(2,1)}), bf16[16,64,1024]{2,1,0:T(8,128)(2,1)}, u32[]{:S(2)}, u32[]{:S(2)}) async-start(bf16[16,64,1024]{2,1,0:T(8,128)(2,1)} %bitcast.12), calls=%async_computation.2 | async-start | bytes 4194304 | tf_op jit(solution)/shard_map/all_to_all | solution.py:105
  77.1 0.2 reduce-scatter.3.cloned.1.call-start
  77.3 0.0 copy-done.1
  77.3 0.1 reshape_squeeze.3
  77.5 0.2 convert_multiply_fusion
  77.7 15.6 %add_multiply_fusion = (f32[1024,2048]{1,0:T(8,128)}, bf16[1024,2048]{1,0:T(8,128)(2,1)}, f32[1024,2048]{1,0:T(8,128)}) fusion(f32[16,2048]{1,0:T(8,128)S(1)} %bitcast.64, bf16[1024,1024]{1,0:T(8,128)(2,1)S(1)} %bitcast.62, bf16[1,1024,2048]{2,1,0:T(8,128)(2,1)} %param.11), kind=kOutput, calls=%fused_computation.14 | convolution fusion | flops 4336910336 | bytes 27394048 | tf_op jit(solution)/shard_map/dot_general | solution.py:21
  93.3 26.3 %all-to-all-done.2 = bf16[16,64,1024]{2,1,0:T(8,128)(2,1)} async-done(((bf16[16,64,1024]{2,1,0:T(8,128)(2,1)}), bf16[16,64,1024]{2,1,0:T(8,128)(2,1)}, u32[]{:S(2)}, u32[]{:S(2)}) %all-to-all-start.2) | async-done | bytes 2097184 | tf_op jit(solution)/shard_map/all_to_all | solution.py:105
  119.6 14.6 %convolution_bitcast_fusion.1 = f32[1024,2048]{1,0:T(8,128)} fusion(bf16[16,64,1024]{2,1,0:T(8,128)(2,1)S(1)} %all-to-all-done, f32[16,64,2048]{2,1,0:T(8,128)} %bitcast.61, bf16[16,64,1024]{2,1,0:T(8,128)(2,1)} %all-to-all-done.2, bf16[1,2048,1024]{2,1,0:T(8,128)(2,1)} %param.12, f32[16,2048]{1,0:T(8,128)S(1)} %bitcast.65), kind=kOutput, calls=%fused_computation.16 | convolution fusion | flops 8596226048 | bytes 25296896 | tf_op jit(solution)/shard_map/dot_general | solution.py:63
  134.2 0.0 reduce-scatter.3.cloned.1.call-update
  134.2 0.3 reduce-scatter.5.cloned.1.call-start
  134.5 12.5 %convolution_bitcast_fusion = f32[2048,1024]{1,0:T(8,128)} fusion(bf16[16,64,1024]{2,1,0:T(8,128)(2,1)} %all-to-all-done.2, f32[16,64,2048]{2,1,0:T(8,128)} %bitcast.60, f32[16,2048]{1,0:T(8,128)S(1)} %bitcast.66), kind=kOutput, calls=%fused_computation.15 | convolution fusion | flops 4299161600 | bytes 19005440 | tf_op jit(solution)/shard_map/dot_general | solution.py:54
  147.0 0.0 reduce-scatter.5.cloned.1.call-update
  147.0 11.6 %fusion.12 = bf16[1024,1024]{1,0:T(8,128)(2,1)} fusion(bf16[1024,2048]{1,0:T(8,128)(2,1)} %get-tuple-element.4, bf16[1,2048,1024]{2,1,0:T(8,128)(2,1)} %param.12), kind=kOutput, calls=%fused_computation.25 | convolution fusion | flops 4296015872 | bytes 10485760 | tf_op jit(solution)/shard_map/dot_general | solution.py:33
  158.6 9.5 %all-to-all-start.1 = ((bf16[16,64,1024]{2,1,0:T(8,128)(2,1)}), bf16[16,64,1024]{2,1,0:T(8,128)(2,1)S(1)}, u32[]{:S(2)}, u32[]{:S(2)}) async-start(bf16[16,64,1024]{2,1,0:T(8,128)(2,1)} %bitcast.63), calls=%async_computation.1 | async-start | bytes 4194304 | tf_op jit(solution)/shard_map/all_to_all | solution.py:103
  168.1 42.6 %all-to-all-done.1 = bf16[16,64,1024]{2,1,0:T(8,128)(2,1)S(1)} async-done(((bf16[16,64,1024]{2,1,0:T(8,128)(2,1)}), bf16[16,64,1024]{2,1,0:T(8,128)(2,1)S(1)}, u32[]{:S(2)}, u32[]{:S(2)}) %all-to-all-start.1) | async-done | bytes 2097184 | tf_op jit(solution)/shard_map/all_to_all | solution.py:103
  210.7 2.0 gather_fusion
  212.7 1.2 multiply_convert_fusion.4
  214.0 0.0 reduce-scatter.3.cloned.1.call-done
  214.0 0.0 reduce-scatter.5.cloned.1.call-done
  (5 shorter events, 0.1 us)
Async XLA Ops:
  7.2 16.8 %copy-start.2 = (f32[512]{0:T(512)S(1)}, f32[512]{0:T(512)}, u32[]{:S(2)}) copy-start(f32[512]{0:T(512)} %param.9) | copy-start | bytes 6148
  7.2 16.8 %copy-start = (bf16[512,1024]{1,0:T(8,128)(2,1)S(1)}, bf16[512,1024]{1,0:T(8,128)(2,1)}, u32[]{:S(2)}) copy-start(bf16[512,1024]{1,0:T(8,128)(2,1)} %param.13) | copy-start | bytes 3145732
  15.6 51.4 %all-to-all-start = ((bf16[16,64,1024]{2,1,0:T(8,128)(2,1)}), bf16[16,64,1024]{2,1,0:T(8,128)(2,1)S(1)}, u32[]{:S(2)}, u32[]{:S(2)}) async-start(bf16[16,64,1024]{2,1,0:T(8,128)(2,1)} %bitcast.5), calls=%async_computation | async-start | bytes 4194304 | tf_op jit(solution)/shard_map/all_to_all | solution.py:99
  24.0 53.3 %copy-start.1 = (s32[1,32,2048]{2,1,0:T(8,128)S(1)}, s32[1,32,2048]{2,1,0:T(8,128)}, u32[]{:S(2)}) copy-start(s32[1,32,2048]{2,1,0:T(8,128)} %param.10) | copy-start | bytes 786436
  67.0 52.6 %all-to-all-start.2 = ((bf16[16,64,1024]{2,1,0:T(8,128)(2,1)}), bf16[16,64,1024]{2,1,0:T(8,128)(2,1)}, u32[]{:S(2)}, u32[]{:S(2)}) async-start(bf16[16,64,1024]{2,1,0:T(8,128)(2,1)} %bitcast.12), calls=%async_computation.2 | async-start | bytes 4194304 | tf_op jit(solution)/shard_map/all_to_all | solution.py:105
  77.1 136.9 %reduce-scatter.3.cloned.1.call-start = ((), (), s32[]{:S(2)}) async-start(), calls=%async_computation.5 | async-start | bytes 12582912 | tf_op jit(solution)/shard_map/reduce_scatter | solution.py:62
  134.2 79.7 %reduce-scatter.5.cloned.1.call-start = ((), (), s32[]{:S(2)}) async-start(), calls=%async_computation.6 | async-start | bytes 12582912 | tf_op jit(solution)/shard_map/reduce_scatter | solution.py:53
  158.6 52.1 %all-to-all-start.1 = ((bf16[16,64,1024]{2,1,0:T(8,128)(2,1)}), bf16[16,64,1024]{2,1,0:T(8,128)(2,1)S(1)}, u32[]{:S(2)}, u32[]{:S(2)}) async-start(bf16[16,64,1024]{2,1,0:T(8,128)(2,1)} %bitcast.63), calls=%async_computation.1 | async-start | bytes 4194304 | tf_op jit(solution)/shard_map/all_to_all | solution.py:103
Sparse Core Ops, SparseCore 0:
  134.4 20.5 reduce-scatter.2
  157.8 17.6 reduce-scatter.4
where the time goes:
time: 225 us; the launch traced here: 221 us
  waiting for transfers between devices  108 us (48%)
  matrix products  54.3 us (24%)
  starting transfers between devices  28.4 us (13%)
  between operations  14.2 us (6%)
  other arithmetic  9.02 us (4%)
  local copies, waits for them, and re-layouts  7.27 us (3%)
    all_to_all x1, waiting for transfers between devices, shards(): lax.all_to_all(out, 'expert', split_axis=0, concat_axis=0, tiled=True)  42.6 us
    all_to_all x1, waiting for transfers between devices, shards(): lax.all_to_all(sent.reshape(n_expert, capacity, width), 'expert', split_a...  38.8 us
    all_to_all x1, waiting for transfers between devices, shards(): lax.all_to_all(sent_grad.reshape(n_expert, capacity, width), 'expert', sp...  26.3 us
    dot_general x1, matrix products, hidden_parts(): jnp.dot(received.reshape(sources * slots, width), weight_in, preferred_el...  15.6 us
    dot_general x1, matrix products, copies_backward(): lax.dot_general(columns, dpre, (((0,), (0,)), ((), ())), preferred_elemen...  14.6 us
    dot_general x1, matrix products, copies_backward(): lax.dot_general(columns, rows_g, (((0,), (0,)), ((), ())), preferred_elem...  12.5 us
    dot_general x1, matrix products, expert_forward(): jnp.dot(hidden.reshape(sources * slots, -1), weight_out, preferred_elemen...  11.6 us
    all_to_all x1, starting transfers between devices, shards(): lax.all_to_all(sent_grad.reshape(n_expert, capacity, width), 'expert', sp...  10.1 us
  transfers between devices with their start and end apart: 5, of which 3 were waited for; matrix products, arithmetic and copies ran while one was open for 22% of the time, Pallas kernels for 0%

commit v1 on v0

--- a/solution.py
+++ b/solution.py
@@ -36,6 +36,26 @@
     return (out.astype(jnp.bfloat16).reshape(sources, slots, width), hidden, slope)
 
 
+def halves_summed(columns, rows):
+    n_replica = lax.axis_size("replica")
+    mine = lax.axis_index("replica")
+    part = columns.shape[1] // n_replica
+
+    def product(owner):
+        block = lax.dynamic_slice_in_dim(columns, owner * part, part, axis=1)
+        return lax.dot_general(
+            block, rows, (((0,), (0,)), ((), ())), preferred_element_type=jnp.float32
+        )
+
+    total = None
+    for shift in range(1, n_replica):
+        ring = [(i, (i + shift) % n_replica) for i in range(n_replica)]
+        came = lax.ppermute(product((mine + shift) % n_replica), "replica", ring)
+        total = came if total is None else total + came
+    own = product(mine)
+    return own if total is None else own + total
+
+
 def copies_backward(received, grad_rows, hidden, slope, keep_scale, weight_out):
     sources, slots, width = received.shape
     hidden_width = weight_out.shape[0]
@@ -49,24 +69,8 @@
         jnp.bfloat16
     )
     dpre = dpre.reshape(sources * slots, hidden_width)
-    columns = flat_hidden
-    grad_out = lax.psum_scatter(
-        lax.dot_general(
-            columns, rows_g, (((0,), (0,)), ((), ())), preferred_element_type=jnp.float32
-        ),
-        "replica",
-        scatter_dimension=0,
-        tiled=True,
-    )
-    columns = rows_x
-    grad_in = lax.psum_scatter(
-        lax.dot_general(
-            columns, dpre, (((0,), (0,)), ((), ())), preferred_element_type=jnp.float32
-        ),
-        "replica",
-        scatter_dimension=0,
-        tiled=True,
-    )
+    grad_out = halves_summed(flat_hidden, rows_g)
+    grad_in = halves_summed(rows_x, dpre)
     return (grad_in, grad_out)
 
 
@@ -100,8 +104,6 @@
         sent.reshape(n_expert, capacity, width), "expert", split_axis=0, concat_axis=0, tiled=True
     )
     out, hidden, slope = expert_forward(received, keep_scale, weight_in, weight_out)
-    back = lax.all_to_all(out, "expert", split_axis=0, concat_axis=0, tiled=True)
-    results = (back, received, hidden, slope)
     grad_rows = lax.all_to_all(
         sent_grad.reshape(n_expert, capacity, width),
         "expert",
@@ -109,10 +111,10 @@
         concat_axis=0,
         tiled=True,
     )
-    returned = results[0]
-    received = results[1]
-    hidden, slope = (results[2], results[3])
+    out, hidden, slope, grad_rows = lax.optimization_barrier((out, hidden, slope, grad_rows))
+    returned = lax.all_to_all(out, "expert", split_axis=0, concat_axis=0, tiled=True)
     grad_in, grad_out = copies_backward(received, grad_rows, hidden, slope, keep_scale, weight_out)
+    returned, grad_in, grad_out = lax.optimization_barrier((returned, grad_in, grad_out))
     expert_out = returned.reshape(n_expert * capacity, width)[target]
     mixed = (router_prob[:, None] * expert_out.astype(jnp.float32)).astype(jnp.bfloat16)
     return (mixed, grad_in[None], grad_out[None])

time: 225 us -> 193 us (0.86)
  the two profiles are of different devices: /device:TPU:0 before, /device:TPU:12 now
where the time goes in v1:
time: 193 us; the launch traced here: 192 us
  waiting for transfers between devices  103 us (53%)
  matrix products  51.9 us (27%)
  starting transfers between devices  17.1 us (9%)
  other arithmetic  12.1 us (6%)
  local copies, waits for them, and re-layouts  7.39 us (4%)
    all_to_all x1, waiting for transfers between devices, shards(): lax.all_to_all(sent.reshape(n_expert, capacity, width), 'expert', split_a...  43.9 us
    all_to_all x1, waiting for transfers between devices, shards(): lax.all_to_all(out, 'expert', split_axis=0, concat_axis=0, tiled=True)  33.6 us
    dot_general x4, matrix products, product(): lax.dot_general(block, rows, (((0,), (0,)), ((), ())), preferred_element_...  26 us
    all_to_all x1, waiting for transfers between devices, shards(): lax.all_to_all(sent_grad.reshape(n_expert, capacity, width), 'expert', sp...  25.6 us
    dot_general x1, matrix products, hidden_parts(): jnp.dot(received.reshape(sources * slots, width), weight_in, preferred_el...  12.8 us
    dot_general x1, matrix products, copies_backward(): lax.dot_general(rows_g, weight_out, (((1,), (1,)), ((), ())), preferred_e...  7.44 us
    all_to_all x1, starting transfers between devices, shards(): lax.all_to_all(sent.reshape(n_expert, capacity, width), 'expert', split_a...  7.17 us
    dot_general x1, matrix products, expert_forward(): jnp.dot(hidden.reshape(sources * slots, -1), weight_out, preferred_elemen...  5.7 us
  transfers between devices with their start and end apart: 5, of which 3 were waited for; matrix products, arithmetic and copies ran while one was open for 27% of the time, Pallas kernels for 0%

profile of v1, /device:TPU:12, one launch (start us, length us, event | category | flops | bytes accessed | tf_op | source)
XLA Modules:
  0.0 192.5 jit_solution(9271301321436125927)
XLA Ops:
  0.6 0.0 copy-start.5
  0.6 0.0 copy-start.7
  0.7 0.8 fusion.33
  1.4 1.1 reduce-window.6
  2.6 0.2 slice_reduce_fusion
  2.8 0.8 fusion.32
  3.6 0.7 compare_select_fusion
  4.3 4.8 %scatter_custom_fusion = bf16[1024,1024]{1,0:T(8,128)(2,1)} fusion(s32[512]{0:T(512)S(1)} %bitcast.73, bf16[512,1024]{1,0:T(8,128)(2,1)} %param.7, bf16[]{:T(256)} %constant.37.clone.1), kind=kCustom, calls=%fused_computation.34 | custom fusion | bytes 2097664 | tf_op jit(solution)/shard_map/scatter | solution.py:91
  9.1 7.2 %all-to-all-start = ((bf16[16,64,1024]{2,1,0:T(8,128)(2,1)}), bf16[16,64,1024]{2,1,0:T(8,128)(2,1)S(1)}, u32[]{:S(2)}, u32[]{:S(2)}) async-start(bf16[16,64,1024]{2,1,0:T(8,128)(2,1)} %bitcast.64), calls=%async_computation | async-start | bytes 4194304 | tf_op jit(solution)/shard_map/all_to_all | solution.py:103
  16.3 0.0 copy-done.5
  16.3 0.0 copy-done.7
  16.3 0.0 copy-start.6
  16.3 4.2 %scatter_custom_fusion.1 = bf16[1024,1024]{1,0:T(8,128)(2,1)} fusion(s32[512]{0:T(512)S(1)} %bitcast.74, bf16[512,1024]{1,0:T(8,128)(2,1)S(1)} %copy-done.5, bf16[]{:T(256)} %constant.37.clone.1, f32[512]{0:T(512)S(1)} %copy-done.7), kind=kCustom, calls=%fused_computation.29 | custom fusion | flops 1572864 | bytes 3147778 | tf_op jit(solution)/shard_map/scatter | solution.py:91
  20.5 43.9 %all-to-all-done = bf16[16,64,1024]{2,1,0:T(8,128)(2,1)S(1)} async-done(((bf16[16,64,1024]{2,1,0:T(8,128)(2,1)}), bf16[16,64,1024]{2,1,0:T(8,128)(2,1)S(1)}, u32[]{:S(2)}, u32[]{:S(2)}) %all-to-all-start) | async-done | bytes 2097184 | tf_op jit(solution)/shard_map/all_to_all | solution.py:103
  64.4 0.0 copy-start
  64.4 4.9 %all-to-all-start.1 = ((bf16[16,64,1024]{2,1,0:T(8,128)(2,1)}), bf16[16,64,1024]{2,1,0:T(8,128)(2,1)}, u32[]{:S(2)}, u32[]{:S(2)}) async-start(bf16[16,64,1024]{2,1,0:T(8,128)(2,1)} %bitcast.63), calls=%async_computation.1 | async-start | bytes 4194304 | tf_op jit(solution)/shard_map/all_to_all | solution.py:107
  69.3 0.0 copy-done.6
  69.3 0.1 reshape_squeeze.3
  69.5 0.1 constant_dynamic-slice_fusion
  69.6 0.1 fusion.30
  69.7 12.8 %fusion.4 = (f32[1024,2048]{1,0:T(8,128)}, bf16[1024,2048]{1,0:T(8,128)(2,1)S(1)}, f32[1024,2048]{1,0:T(8,128)S(1)}) fusion(f32[16,2048]{1,0:T(8,128)S(1)} %fusion.30, bf16[1024,1024]{1,0:T(8,128)(2,1)S(1)} %bitcast.59, bf16[1,1024,2048]{2,1,0:T(8,128)(2,1)} %param.11), kind=kOutput, calls=%fused_computation.9 | convolution fusion | flops 4336910336 | bytes 27394048 | tf_op jit(solution)/shard_map/dot_general | solution.py:21
  82.5 0.0 copy-start.8
  82.5 3.2 %multiply_convert_fusion.1 = bf16[16,64,2048]{2,1,0:T(8,128)(2,1)} fusion(f32[16,64,2048]{2,1,0:T(8,128)S(1)} %bitcast.58, f32[16,2048]{1,0:T(8,128)S(1)} %fusion.30), kind=kLoop, calls=%fused_computation.13 | loop fusion | flops 4194304 | bytes 12713984 | tf_op jit(solution)/shard_map/convert_element_type | solution.py:26
  85.8 0.0 copy-done.8
  85.8 5.7 %fusion.18 = bf16[1024,1024]{1,0:T(8,128)(2,1)} fusion(bf16[1024,2048]{1,0:T(8,128)(2,1)S(1)} %get-tuple-element.18, bf16[1,2048,1024]{2,1,0:T(8,128)(2,1)S(1)} %copy-done.8), kind=kOutput, calls=%fused_computation.28 | convolution fusion | flops 4296015872 | bytes 10485760 | tf_op jit(solution)/shard_map/dot_general | solution.py:33
  91.5 25.6 %all-to-all-done.1 = bf16[16,64,1024]{2,1,0:T(8,128)(2,1)} async-done(((bf16[16,64,1024]{2,1,0:T(8,128)(2,1)}), bf16[16,64,1024]{2,1,0:T(8,128)(2,1)}, u32[]{:S(2)}, u32[]{:S(2)}) %all-to-all-start.1) | async-done | bytes 2097184 | tf_op jit(solution)/shard_map/all_to_all | solution.py:107
  117.1 0.0 copy-start.2
  117.1 6.8 %fusion.11 = f32[1024,1024]{1,0:T(8,128)} fusion(bf16[1024,1024]{1,0:T(8,128)(2,1)} %bitcast.18, bf16[1024,2048]{1,0:T(8,128)(2,1)} %bitcast.67, s32[]{:T(128)S(6)} %select_n.64), kind=kOutput, calls=%fused_computation.22 | convolution fusion | flops 2147483648 | bytes 8388612 | tf_op jit(solution)/shard_map/dot_general | solution.py:46
  123.9 0.0 collective-permute-start.1
  123.9 0.0 copy-done.2
  123.9 7.4 %multiply_convert_fusion = bf16[16,64,2048]{2,1,0:T(8,128)(2,1)S(1)} fusion(f32[16,64,2048]{2,1,0:T(8,128)S(1)} %bitcast.62, bf16[16,64,1024]{2,1,0:T(8,128)(2,1)} %all-to-all-done.1, bf16[1,2048,1024]{2,1,0:T(8,128)(2,1)} %param.12, f32[16,2048]{1,0:T(8,128)S(1)} %fusion.30), kind=kOutput, calls=%fused_computation.12 | convolution fusion | flops 4301258752 | bytes 19005440 | tf_op jit(solution)/shard_map/dot_general | solution.py:65
  131.3 0.0 copy-start.3
  131.3 0.0 copy-done
  131.4 4.5 %fusion.22 = f32[512,2048]{1,0:T(8,128)} fusion(bf16[1024,2048]{1,0:T(8,128)(2,1)S(1)} %bitcast.65, bf16[1024,1024]{1,0:T(8,128)(2,1)S(1)} %bitcast.60, s32[]{:T(128)S(6)} %select_n.62), kind=kOutput, calls=%fused_computation.30 | convolution fusion | flops 2147483648 | bytes 9437188 | tf_op jit(solution)/shard_map/dot_general | solution.py:46
  135.8 0.0 copy-done.3
  135.8 0.5 collective-permute-start
  136.3 4.5 %all-to-all-start.2 = ((bf16[16,64,1024]{2,1,0:T(8,128)(2,1)}), bf16[16,64,1024]{2,1,0:T(8,128)(2,1)S(1)}, u32[]{:S(2)}, u32[]{:S(2)}) async-start(bf16[16,64,1024]{2,1,0:T(8,128)(2,1)} %bitcast.70), calls=%async_computation.2 | async-start | bytes 4194304 | tf_op jit(solution)/shard_map/all_to_all | solution.py:115
  140.9 0.0 copy-start.1
  140.9 0.0 copy-start.4
  140.9 0.0 collective-permute-done.1
  140.9 8.0 %fusion.15 = f32[1024,1024]{1,0:T(8,128)} fusion(f32[1024,1024]{1,0:T(8,128)} %collective-permute-done.1, bf16[1024,1024]{1,0:T(8,128)(2,1)} %bitcast.18, bf16[1024,2048]{1,0:T(8,128)(2,1)} %bitcast.68, s32[]{:T(128)S(6)} %select_n.63), kind=kOutput, calls=%fused_computation.27 | convolution fusion | flops 2148532224 | bytes 12582916 | tf_op jit(solution)/shard_map/dot_general | solution.py:46
  148.9 0.0 collective-permute-done
  148.9 0.0 copy-done.1
  148.9 0.0 copy-done.4
  148.9 6.7 %convolution_add_fusion = f32[512,2048]{1,0:T(8,128)} fusion(f32[512,2048]{1,0:T(8,128)} %collective-permute-done, bf16[1024,2048]{1,0:T(8,128)(2,1)S(1)} %bitcast.66, bf16[1024,1024]{1,0:T(8,128)(2,1)S(1)} %bitcast.61, s32[]{:T(128)S(6)} %select_n.60), kind=kOutput, calls=%fused_computation.20 | convolution fusion | flops 2148532224 | bytes 13631492 | tf_op jit(solution)/shard_map/dot_general | solution.py:46
  155.6 33.6 %all-to-all-done.2 = bf16[16,64,1024]{2,1,0:T(8,128)(2,1)S(1)} async-done(((bf16[16,64,1024]{2,1,0:T(8,128)(2,1)}), bf16[16,64,1024]{2,1,0:T(8,128)(2,1)S(1)}, u32[]{:S(2)}, u32[]{:S(2)}) %all-to-all-start.2) | async-done | bytes 2097184 | tf_op jit(solution)/shard_map/all_to_all | solution.py:115
  189.2 2.0 %gather_fusion = bf16[512,1024]{1,0:T(8,128)(2,1)S(1)} fusion(bf16[1024,1024]{1,0:T(8,128)(2,1)S(1)} %bitcast.57, s32[1024]{0:T(1024)S(1)} %pad_clamp_fusion), kind=kCustom, calls=%fused_computation | custom fusion | bytes 2099200 | tf_op jit(solution)/shard_map/gather | solution.py:118
  191.3 1.2 multiply_convert_fusion.2
  (4 shorter events, 0.1 us)
Async XLA Ops:
  0.6 15.6 %copy-start.5 = (bf16[512,1024]{1,0:T(8,128)(2,1)S(1)}, bf16[512,1024]{1,0:T(8,128)(2,1)}, u32[]{:S(2)}) copy-start(bf16[512,1024]{1,0:T(8,128)(2,1)} %param.13) | copy-start | bytes 3145732
  0.6 15.6 %copy-start.7 = (f32[512]{0:T(512)S(1)}, f32[512]{0:T(512)}, u32[]{:S(2)}) copy-start(f32[512]{0:T(512)} %param.9) | copy-start | bytes 6148
  9.1 55.3 %all-to-all-start = ((bf16[16,64,1024]{2,1,0:T(8,128)(2,1)}), bf16[16,64,1024]{2,1,0:T(8,128)(2,1)S(1)}, u32[]{:S(2)}, u32[]{:S(2)}) async-start(bf16[16,64,1024]{2,1,0:T(8,128)(2,1)} %bitcast.64), calls=%async_computation | async-start | bytes 4194304 | tf_op jit(solution)/shard_map/all_to_all | solution.py:103
  16.3 53.0 %copy-start.6 = (s32[1,32,2048]{2,1,0:T(8,128)S(1)}, s32[1,32,2048]{2,1,0:T(8,128)}, u32[]{:S(2)}) copy-start(s32[1,32,2048]{2,1,0:T(8,128)} %param.10) | copy-start | bytes 786436
  64.4 66.9 %copy-start = (bf16[16,64,1024]{2,1,0:T(8,128)(2,1)}, bf16[16,64,1024]{2,1,0:T(8,128)(2,1)S(1)}, u32[]{:S(2)}) copy-start(bf16[16,64,1024]{2,1,0:T(8,128)(2,1)S(1)} %all-to-all-done) | copy-start | bytes 6291460
  64.4 52.7 %all-to-all-start.1 = ((bf16[16,64,1024]{2,1,0:T(8,128)(2,1)}), bf16[16,64,1024]{2,1,0:T(8,128)(2,1)}, u32[]{:S(2)}, u32[]{:S(2)}) async-start(bf16[16,64,1024]{2,1,0:T(8,128)(2,1)} %bitcast.63), calls=%async_computation.1 | async-start | bytes 4194304 | tf_op jit(solution)/shard_map/all_to_all | solution.py:107
  82.5 3.2 %copy-start.8 = (bf16[1,2048,1024]{2,1,0:T(8,128)(2,1)S(1)}, bf16[1,2048,1024]{2,1,0:T(8,128)(2,1)}, u32[]{:S(2)}) copy-start(bf16[1,2048,1024]{2,1,0:T(8,128)(2,1)} %param.12) | copy-start | bytes 12582916
  117.1 6.8 %copy-start.2 = (f32[1024,2048]{1,0:T(8,128)S(1)}, f32[1024,2048]{1,0:T(8,128)}, u32[]{:S(2)}) copy-start(f32[1024,2048]{1,0:T(8,128)} %get-tuple-element.17) | copy-start | bytes 25165828
  123.9 17.0 %collective-permute-start.1 = (f32[1024,1024]{1,0:T(8,128)}, f32[1024,1024]{1,0:T(8,128)}, u32[]{:S(2)}, u32[]{:S(2)}) collective-permute-start(f32[1024,1024]{1,0:T(8,128)} %fusion.11), channel_id=1, source_target_pairs={{0,1},{1,0},{2,3},{3,2},{4,5},{5,4},{6,7},{7,6},{8,9},{9,8},{10,11... | collective-permute-start | bytes 12582920 | tf_op jit(solution)/shard_map/ppermute | solution.py:53
  131.3 4.5 %copy-start.3 = (bf16[16,64,2048]{2,1,0:T(8,128)(2,1)}, bf16[16,64,2048]{2,1,0:T(8,128)(2,1)S(1)}, u32[]{:S(2)}) copy-start(bf16[16,64,2048]{2,1,0:T(8,128)(2,1)S(1)} %multiply_convert_fusion) | copy-start | bytes 12582916
  135.8 13.1 %collective-permute-start = (f32[512,2048]{1,0:T(8,128)}, f32[512,2048]{1,0:T(8,128)}, u32[]{:S(2)}, u32[]{:S(2)}) collective-permute-start(f32[512,2048]{1,0:T(8,128)} %fusion.22), channel_id=1, source_target_pairs={{0,1},{1,0},{2,3},{3,2},{4,5},{5,4},{6,7},{7,6},{8,9},{9,8},{10,11... | collective-permute-start | bytes 12582920 | tf_op jit(solution)/shard_map/ppermute | solution.py:53
  136.3 52.9 %all-to-all-start.2 = ((bf16[16,64,1024]{2,1,0:T(8,128)(2,1)}), bf16[16,64,1024]{2,1,0:T(8,128)(2,1)S(1)}, u32[]{:S(2)}, u32[]{:S(2)}) async-start(bf16[16,64,1024]{2,1,0:T(8,128)(2,1)} %bitcast.70), calls=%async_computation.2 | async-start | bytes 4194304 | tf_op jit(solution)/shard_map/all_to_all | solution.py:115
  140.9 8.0 %copy-start.1 = (bf16[16,64,1024]{2,1,0:T(8,128)(2,1)S(1)}, bf16[16,64,1024]{2,1,0:T(8,128)(2,1)}, u32[]{:S(2)}) copy-start(bf16[16,64,1024]{2,1,0:T(8,128)(2,1)} %copy-done) | copy-start | bytes 6291460
  140.9 8.0 %copy-start.4 = (bf16[16,64,2048]{2,1,0:T(8,128)(2,1)S(1)}, bf16[16,64,2048]{2,1,0:T(8,128)(2,1)}, u32[]{:S(2)}) copy-start(bf16[16,64,2048]{2,1,0:T(8,128)(2,1)} %copy-done.3) | copy-start | bytes 12582916

commit v2 on v0

v2 whole, which is shorter than its diff:
```python
import functools

import jax
import jax.numpy as jnp
from jax import lax
from jax.experimental import pallas as pl
from jax.experimental.pallas import tpu as pltpu
from jax.sharding import PartitionSpec as P

KEEP_SCALE = 4.0 / 3.0
MESH = pl.DeviceIdType.MESH


def gelu_parts(pre):
    inner = 0.7978845608 * (pre + 0.044715 * pre * pre * pre)
    tanh_v = jnp.tanh(inner)
    value = 0.5 * pre * (1.0 + tanh_v)
    slope = 0.5 * (1.0 + tanh_v) + 0.5 * pre * (1.0 - tanh_v * tanh_v) * 0.7978845608 * (
        1.0 + 3.0 * 0.044715 * pre * pre
    )
    return (value, slope)


def tile_of(size, most):
    return size if size <= most else most


def kernel(
    n, group,
    sent, sent_grad, keep, w_in, w_out,
    back, grad_in, grad_out,
    weight_in, weight_out, rows_x, rows_g, rows_o, hidden, factor, dpre,
    give_out, came_out, give_in, came_in,
    weight_sem, own_sem, x_send, x_recv, g_send, g_recv, o_send, o_recv, pair_send, pair_recv, done_sem,
):
    me = lax.axis_index("expert")
    core = lax.axis_index("replica")
    other = 1 - core
    cap, width = rows_x.shape[1:]
    ff = weight_in.shape[1]
    rows = group * cap
    groups = n // group
    tile = tile_of(ff, 512)
    wide = tile_of(width, 256)

    def weight_copy(i):
        source, target = ((w_in, weight_in), (w_out, weight_out))[i]
        return pltpu.make_async_copy(source, target, weight_sem.at[i])

    weight_copy(0).start()
    weight_copy(1).start()

    def own_copy(i):
        source, target = (
            (sent.at[me], rows_x.at[0]), (sent_grad.at[me], rows_g.at[0]), (rows_o.at[0], back.at[me])
        )[i]
        return pltpu.make_async_copy(source, target, own_sem.at[i])

    def ahead(k):
        return lax.rem(me + k, n)

    def behind(k):
        return lax.rem(me - k + n, n)

    def x_copy(k):
        return pltpu.make_async_remote_copy(
            src_ref=sent.at[ahead(k)], dst_ref=rows_x.at[k], send_sem=x_send.at[k],
            recv_sem=x_recv.at[k], device_id=(ahead(k), core), device_id_type=MESH,
        )

    def g_copy(k):
        return pltpu.make_async_remote_copy(
            src_ref=sent_grad.at[ahead(k)], dst_ref=rows_g.at[k], send_sem=g_send.at[k],
            recv_sem=g_recv.at[k], device_id=(ahead(k), core), device_id_type=MESH,
        )

    def o_copy(k):
        return pltpu.make_async_remote_copy(
            src_ref=rows_o.at[k], dst_ref=back.at[me], send_sem=o_send.at[k],
            recv_sem=o_recv.at[k], device_id=(behind(k), core), device_id_type=MESH,
        )

    def pair_copy(i):
        source, target = ((give_out, came_out), (give_in, came_in))[i]
        return pltpu.make_async_remote_copy(
            src_ref=source, dst_ref=target, send_sem=pair_send.at[i],
            recv_sem=pair_recv.at[i], device_id=(me, other), device_id_type=MESH,
        )

    def result_copy(i):
        source, target = ((came_out, grad_out), (came_in, grad_in))[i]
        return pltpu.make_async_copy(source, target, done_sem.at[i])

    def each(low, high, step):
        def run(i, carry):
            step(i)
            return carry

        lax.fori_loop(low, high, run, 0)

    own_copy(0).start()
    own_copy(1).start()
    barrier = pltpu.get_barrier_semaphore()

    def greet(k):
        pl.semaphore_signal(barrier, inc=1, device_id=(ahead(k), core), device_id_type=MESH)

    each(1, n, greet)
    pl.semaphore_signal(barrier, inc=1, device_id=(me, other), device_id_type=MESH)
    pl.semaphore_wait(barrier, n)

    each(1, n, lambda k: x_copy(k).start())
    each(1, n, lambda k: g_copy(k).start())
    own_copy(0).wait()
    own_copy(1).wait()
    weight_copy(0).wait()
    weight_copy(1).wait()

    def forward(g):
        first = g * group

        def arrived(k):
            @pl.when(k > 0)
            def _():
                x_copy(k).wait_recv()

        each(first, first + group, arrived)

        def project(j):
            columns = pl.ds(pl.multiple_of(j * tile, tile), tile)
            block = rows_x[pl.ds(first, group)].reshape(rows, width)
            pre = jnp.dot(block, weight_in[:, columns], preferred_element_type=jnp.float32)
            value, slope = gelu_parts(pre)
            scale = keep[pl.ds(first, group), :, columns]
            value = value.reshape(group, cap, tile) * scale
            slope = slope.reshape(group, cap, tile) * scale
            hidden[pl.ds(first, group), :, columns] = value.astype(jnp.bfloat16)
            factor[pl.ds(first, group), :, columns] = slope

        each(0, ff // tile, project)

        def output(j):
            columns = pl.ds(pl.multiple_of(j * wide, wide), wide)
            block = hidden[pl.ds(first, group)].reshape(rows, ff)
            out = jnp.dot(block, weight_out[:, columns], preferred_element_type=jnp.float32)
            rows_o[pl.ds(first, group), :, columns] = out.astype(jnp.bfloat16).reshape(group, cap, wide)

        each(0, width // wide, output)

        def give_back(k):
            @pl.when(k > 0)
            def _():
                o_copy(k).start()

            @pl.when(k == 0)
            def _():
                own_copy(2).start()

        each(first, first + group, give_back)

    each(0, groups, forward)

    def backward(g):
        first = g * group

        def arrived(k):
            @pl.when(k > 0)
            def _():
                g_copy(k).wait_recv()

        each(first, first + group, arrived)

        def pull(j):
            columns = pl.ds(pl.multiple_of(j * tile, tile), tile)
            block = rows_g[pl.ds(first, group)].reshape(rows, width)
            dhidden = lax.dot_general(
                block, weight_out[columns, :], (((1,), (1,)), ((), ())),
                preferred_element_type=jnp.float32,
            )
            dhidden = dhidden.reshape(group, cap, tile) * factor[pl.ds(first, group), :, columns]
            dpre[pl.ds(first, group), :, columns] = dhidden.astype(jnp.bfloat16)

        each(0, ff // tile, pull)

    each(0, groups, backward)

    def product(left, right, start, j, part):
        columns = pl.ds(pl.multiple_of(start + j * part, part), part)
        return lax.dot_general(
            left[:, :, columns].reshape(n * cap, part), right[...].reshape(n * cap, right.shape[2]),
            (((0,), (0,)), ((), ())), preferred_element_type=jnp.float32,
        )

    def gradient(i, left, right, give, came):
        half = give.shape[0]
        part = tile_of(half, 128)

        def theirs(j):
            give[pl.ds(pl.multiple_of(j * part, part), part), :] = product(
                left, right, other * half, j, part)

        def mine(j):
            spot = pl.ds(pl.multiple_of(j * part, part), part)
            came[spot, :] += product(left, right, core * half, j, part)

        return functools.partial(each, 0, half // part, theirs), functools.partial(each, 0, half // part, mine)

    theirs_out, mine_out = gradient(0, hidden, rows_g, give_out, came_out)
    theirs_in, mine_in = gradient(1, rows_x, dpre, give_in, came_in)
    theirs_out()
    pair_copy(0).start()
    theirs_in()
    pair_copy(1).start()
    pair_copy(0).wait_recv()
    mine_out()
    result_copy(0).start()
    pair_copy(1).wait_recv()
    mine_in()
    result_copy(1).start()

    own_copy(2).wait()

    def finish(k):
        x_copy(k).wait_send()
        g_copy(k).wait_send()
        o_copy(k).wait_send()
        o_copy(k).wait_recv()

    each(1, n, finish)
    pair_copy(0).wait_send()
    pair_copy(1).wait_send()
    result_copy(0).wait()
    result_copy(1).wait()


def exchange(sent, sent_grad, keep, w_in, w_out):
    n, cap, width = sent.shape
    ff = w_in.shape[1]
    group = min(n, max(1, 256 // cap))
    dma = pltpu.SemaphoreType.DMA
    f32, bf16 = jnp.float32, jnp.bfloat16
    whole = pl.BlockSpec(memory_space=pl.ANY)
    flops = 10 * n * cap * width * ff
    return pl.pallas_call(
        functools.partial(kernel, n, group),
        out_shape=(
            jax.ShapeDtypeStruct((n, cap, width), bf16),
            jax.ShapeDtypeStruct((width // 2, ff), f32),
            jax.ShapeDtypeStruct((ff // 2, width), f32),
        ),
        in_specs=[whole, whole, pl.BlockSpec(memory_space=pltpu.VMEM), whole, whole],
        out_specs=(whole, whole, whole),
        scratch_shapes=[
            pltpu.VMEM((width, ff), bf16),
            pltpu.VMEM((ff, width), bf16),
            pltpu.VMEM((n, cap, width), bf16),
            pltpu.VMEM((n, cap, width), bf16),
            pltpu.VMEM((n, cap, width), bf16),
            pltpu.VMEM((n, cap, ff), bf16),
            pltpu.VMEM((n, cap, ff), f32),
            pltpu.VMEM((n, cap, ff), bf16),
            pltpu.VMEM((ff // 2, width), f32),
            pltpu.VMEM((ff // 2, width), f32),
            pltpu.VMEM((width // 2, ff), f32),
            pltpu.VMEM((width // 2, ff), f32),
            dma((2,)), dma((3,)), dma((n,)), dma((n,)), dma((n,)), dma((n,)), dma((n,)), dma((n,)),
            dma((2,)), dma((2,)), dma((2,)),
        ],
        cost_estimate=pl.CostEstimate(flops=flops, bytes_accessed=40 << 20, transcendentals=n * cap * ff),
        compiler_params=pltpu.CompilerParams(
            collective_id=0, has_side_effects=True, vmem_limit_bytes=60 << 20
        ),
    )(sent, sent_grad, keep, w_in, w_out)


def shards(tokens, expert_id, router_prob, keep_mask, w_in, w_out, cotangent):
    tok_rows, width = tokens.shape
    n_expert = lax.axis_size("expert")
    n_replica = lax.axis_size("replica")
    capacity = 2 * tok_rows // n_expert
    portion = capacity // n_replica
    weight_in = w_in[0]
    weight_out = w_out[0]
    ids = expert_id[:, 0]
    onehot = (ids[:, None] == jnp.arange(n_expert, dtype=jnp.int32)[None, :]).astype(jnp.int32)
    ranks = jnp.sum(jnp.cumsum(onehot, axis=0) * onehot, axis=1) - 1
    target = ids * capacity + ranks % n_replica * portion + ranks // n_replica

    def fill_slots(values):
        return jnp.zeros((n_expert * capacity, width), values.dtype).at[target].set(values)

    sent = fill_slots(tokens)
    gated = (router_prob[:, None] * cotangent.astype(jnp.float32)).astype(jnp.bfloat16)
    sent_grad = fill_slots(gated)
    keep_rows = lax.dynamic_index_in_dim(
        keep_mask[0].reshape(n_expert, n_replica, -1),
        lax.axis_index("replica"),
        axis=1,
        keepdims=False,
    )
    keep_scale = keep_rows.astype(jnp.float32) * KEEP_SCALE
    sources = (lax.axis_index("expert") - jnp.arange(n_expert) + n_expert) % n_expert
    keep_scale = keep_scale[sources][:, None, :]
    returned, grad_in, grad_out = exchange(
        sent.reshape(n_expert, capacity, width),
        sent_grad.reshape(n_expert, capacity, width),
        keep_scale,
        weight_in,
        weight_out,
    )
    expert_out = returned.reshape(n_expert * capacity, width)[target]
    mixed = (router_prob[:, None] * expert_out.astype(jnp.float32)).astype(jnp.bfloat16)
    return (mixed, grad_in[None], grad_out[None])


def solution(mesh):
    in_specs = (
        P(("expert", "replica"), None),
        P(("expert", "replica"), None),
        P(("expert", "replica")),
        P("expert", None, None),
        P("expert", None, None),
        P("expert", None, None),
        P(("expert", "replica"), None),
    )
    out_specs = (
        P(("expert", "replica"), None),
        P("expert", "replica", None),
        P("expert", "replica", None),
    )
    return jax.shard_map(shards, mesh=mesh, in_specs=in_specs, out_specs=out_specs, check_vma=False)
```

time: 225 us -> 180 us (0.80); the launches traced: 221 us -> 180 us
  Pallas kernels: 0 us -> 153 us
  waiting for transfers between devices: 108 us -> 0 us
  matrix products: 54.3 us -> 0 us
  starting transfers between devices: 28.4 us -> 0 us
  between operations: 14.2 us -> 0.75 us
  local copies, waits for them, and re-layouts: 7.27 us -> 19.1 us
    pallas_call x0 -> x1, Pallas kernels: none -> 153 us  [exchange(): pl.pallas_call(functools.partial(kernel, n, group), out_shape=(jax.ShapeD...]
    all_to_all x3 -> x0, waiting for transfers between devices: 108 us -> none  [the longest x1 42.6 us: shards(): lax.all_to_all(out, 'expert', split_axis=0, concat_axis=0, tiled=True)]
    dot_general x4 -> x0, matrix products: 54.3 us -> none  [the longest x1 15.6 us: hidden_parts(): jnp.dot(received.reshape(sources * slots, width), weight_in, preferred_el...]
    all_to_all x3 -> x0, starting transfers between devices: 27.9 us -> none  [the longest x1 10.1 us: shards(): lax.all_to_all(sent_grad.reshape(n_expert, capacity, width), 'expert', sp...]
    unnamed x7 -> x10, local copies, waits for them, and re-layouts: 0.06 us -> 6.88 us
    gather x1, local copies, waits for them, and re-layouts: 2.05 us -> 4.59 us  [shards(): expert_out = returned.reshape(n_expert * capacity, width)[target]]
  transfers between devices with their start and end apart: 5 -> 0, of which waited for: 3 -> 0; matrix products, arithmetic and copies ran while one was open for 22% -> 0% of each run, Pallas kernels for 0% -> 0%
where the time goes in v2:
time: 180 us
  Pallas kernels  153 us (85%)
  local copies, waits for them, and re-layouts  19.1 us (11%)
  other arithmetic  6.8 us (4%)
    pallas_call x1, Pallas kernels, exchange(): pl.pallas_call(functools.partial(kernel, n, group), out_shape=(jax.ShapeD...  153 us
    unnamed x10, local copies, waits for them, and re-layouts  6.88 us
    scatter x1, local copies, waits for them, and re-layouts, fill_slots(): jnp.zeros((n_expert * capacity, width), values.dtype).at[target].set(values)  4.79 us
    gather x1, local copies, waits for them, and re-layouts, shards(): expert_out = returned.reshape(n_expert * capacity, width)[target]  4.59 us
    scatter x1, other arithmetic, fill_slots(): jnp.zeros((n_expert * capacity, width), values.dtype).at[target].set(values)  4.19 us

profile of v2, /device:TPU:0, one launch (start us, length us, event | category | flops | bytes accessed | tf_op | source)
XLA Modules:
  0.0 179.6 jit_solution(1045024357401844161)
XLA Ops:
  0.6 0.0 copy-start.2
  0.6 1.1 reshape_squeeze.3
  1.7 0.0 copy-start.1
  1.8 0.0 copy-start.3
  1.8 0.1 constant_dynamic-slice_fusion
  1.9 0.1 fusion.6
  2.0 0.6 gather_fusion
  2.6 0.7 broadcast_in_dim.6.keep
  3.4 0.0 copy-done.2
  3.4 1.2 reduce-window.6
  4.5 0.2 slice_reduce_fusion
  4.8 0.1 fusion.8
  4.9 4.8 %scatter_custom_fusion = bf16[1024,1024]{1,0:T(8,128)(2,1)} fusion(s32[512]{0:T(512)S(1)} %bitcast.37, bf16[512,1024]{1,0:T(8,128)(2,1)} %param.7, bf16[]{:T(256)} %constant.59.clone.1), kind=kCustom, calls=%fused_computation.8 | custom fusion | bytes 2097664 | tf_op jit(solution)/shard_map/scatter | solution.py:290
  9.7 0.0 copy-done.1
  9.7 0.0 copy-done.3
  9.7 4.2 %scatter_custom_fusion.1 = bf16[1024,1024]{1,0:T(8,128)(2,1)} fusion(s32[512]{0:T(512)S(1)} %bitcast.38, bf16[512,1024]{1,0:T(8,128)(2,1)S(1)} %copy-done.1, bf16[]{:T(256)} %constant.59.clone.1, f32[512]{0:T(512)S(1)} %copy-done.3), kind=kCustom, calls=%fused_computation.6 | custom fusion | flops 1572864 | bytes 3147778 | tf_op jit(solution)/shard_map/scatter | solution.py:290
  13.9 153.0 %shard_map.94 = (bf16[16,64,1024]{2,1,0:T(8,128)(2,1)}, f32[512,2048]{1,0:T(8,128)}, f32[1024,1024]{1,0:T(8,128)}) custom-call(bf16[16,64,1024]{2,1,0:T(8,128)(2,1)} %bitcast.33, bf16[16,64,1024]{2,1,0:T(8,128)(2,1)} %bitcast.34, f32[16,1,2048]{2,1,0:T(1,128)} %broadcast_in_dim.6.keep, bf16[1024,2048]{1,0:T(8,128)(2,1)} %bitcast.41, bf16[2048,1024]{1,0:T(8,128)(2,1)} %bitcast.42), custom_call_target="tpu_custom_call" | custom-call | flops 21474836480 | bytes 41943040 | tf_op jit(solution)/shard_map/pallas_call | solution.py:244
  166.9 4.6 %gather_fusion.1 = bf16[512,1024]{1,0:T(8,128)(2,1)S(1)} fusion(bf16[1024,1024]{1,0:T(8,128)(2,1)} %bitcast.30, s32[1024]{0:T(1024)S(1)} %pad_clamp_fusion), kind=kCustom, calls=%fused_computation.1 | custom fusion | bytes 2099200 | tf_op jit(solution)/shard_map/gather | solution.py:311
  171.5 1.2 multiply_convert_fusion
  172.7 0.0 copy-start
  172.7 4.8 %copy.22 = f32[1,512,2048]{2,1,0:T(8,128)} copy(f32[1,512,2048]{2,1,0:T(8,128)} %bitcast.32) | data formatting | bytes 8388608
  177.6 0.0 copy-done
  177.6 2.0 %copy.23 = f32[1,1024,1024]{2,1,0:T(8,128)} copy(f32[1,1024,1024]{2,1,0:T(8,128)S(1)} %bitcast.31) | data formatting | bytes 8388608
  (8 shorter events, 0.1 us)
Async XLA Ops:
  0.6 2.7 %copy-start.2 = (s32[512,1]{0,1:T(1,128)S(1)}, s32[512,1]{0,1:T(1,128)}, u32[]{:S(2)}) copy-start(s32[512,1]{0,1:T(1,128)} %param.8) | copy-start | bytes 6148
  1.7 8.0 %copy-start.1 = (bf16[512,1024]{1,0:T(8,128)(2,1)S(1)}, bf16[512,1024]{1,0:T(8,128)(2,1)}, u32[]{:S(2)}) copy-start(bf16[512,1024]{1,0:T(8,128)(2,1)} %param.13) | copy-start | bytes 3145732
  1.8 8.0 %copy-start.3 = (f32[512]{0:T(512)S(1)}, f32[512]{0:T(512)}, u32[]{:S(2)}) copy-start(f32[512]{0:T(512)} %param.9) | copy-start | bytes 6148
  172.7 4.9 %copy-start = (f32[1024,1024]{1,0:T(8,128)S(1)}, f32[1024,1024]{1,0:T(8,128)}, u32[]{:S(2)}) copy-start(f32[1024,1024]{1,0:T(8,128)} %get-tuple-element.8) | copy-start | bytes 12582916

commit v3 on v2

--- a/solution.py
+++ b/solution.py
@@ -27,10 +27,11 @@
 
 def kernel(
     n, group,
-    sent, sent_grad, keep, w_in, w_out,
-    back, grad_in, grad_out,
+    tokens, cotangent, prob, slot_row, slot_column, keep, w_in, w_out,
+    mixed, grad_in, grad_out,
+    sent, sent_grad, back,
     weight_in, weight_out, rows_x, rows_g, rows_o, hidden, factor, dpre,
-    give_out, came_out, give_in, came_in,
+    give_out, came_out, came_in,
     weight_sem, own_sem, x_send, x_recv, g_send, g_recv, o_send, o_recv, pair_send, pair_recv, done_sem,
 ):
     me = lax.axis_index("expert")
@@ -42,6 +43,8 @@
     groups = n // group
     tile = tile_of(ff, 512)
     wide = tile_of(width, 256)
+    count = tokens.shape[0]
+    give_in = factor.at[pl.ds(0, came_in.shape[0])]
 
     def weight_copy(i):
         source, target = ((w_in, weight_in), (w_out, weight_out))[i]
@@ -52,7 +55,7 @@
 
     def own_copy(i):
         source, target = (
-            (sent.at[me], rows_x.at[0]), (sent_grad.at[me], rows_g.at[0]), (rows_o.at[0], back.at[me])
+            (sent.at[0], rows_x.at[0]), (sent_grad.at[0], rows_g.at[0]), (rows_o.at[0], back.at[me])
         )[i]
         return pltpu.make_async_copy(source, target, own_sem.at[i])
 
@@ -64,13 +67,13 @@
 
     def x_copy(k):
         return pltpu.make_async_remote_copy(
-            src_ref=sent.at[ahead(k)], dst_ref=rows_x.at[k], send_sem=x_send.at[k],
+            src_ref=sent.at[k], dst_ref=rows_x.at[k], send_sem=x_send.at[k],
             recv_sem=x_recv.at[k], device_id=(ahead(k), core), device_id_type=MESH,
         )
 
     def g_copy(k):
         return pltpu.make_async_remote_copy(
-            src_ref=sent_grad.at[ahead(k)], dst_ref=rows_g.at[k], send_sem=g_send.at[k],
+            src_ref=sent_grad.at[k], dst_ref=rows_g.at[k], send_sem=g_send.at[k],
             recv_sem=g_recv.at[k], device_id=(ahead(k), core), device_id_type=MESH,
         )
 
@@ -98,8 +101,6 @@
 
         lax.fori_loop(low, high, run, 0)
 
-    own_copy(0).start()
-    own_copy(1).start()
     barrier = pltpu.get_barrier_semaphore()
 
     def greet(k):
@@ -107,17 +108,50 @@
 
     each(1, n, greet)
     pl.semaphore_signal(barrier, inc=1, device_id=(me, other), device_id_type=MESH)
+
+    def dispatch(values, slots):
+        def fill(g):
+            first = g * group
+            shape = (group, cap, count)
+            expert = lax.broadcasted_iota(jnp.int32, shape, 0) + (first + me)
+            expert = jnp.where(expert >= n, expert - n, expert)
+            place = expert * cap + lax.broadcasted_iota(jnp.int32, shape, 1)
+            chosen = jnp.where(place == slot_row[...][None], 1.0, 0.0).astype(jnp.bfloat16)
+            filled = jnp.dot(
+                chosen.reshape(rows, count), values[...], preferred_element_type=jnp.float32
+            )
+            slots[pl.ds(first, group)] = filled.astype(jnp.bfloat16).reshape(group, cap, width)
+
+        each(0, groups, fill)
+
+    def later(copy):
+        def start(i):
+            k = lax.rem((1 - core) * (i + n // 4) + core * (n // 4 * 3 - 1 - i + n), n)
+
+            @pl.when(k > 0)
+            def _():
+                copy(k).start()
+
+        return start
+
+    dispatch(tokens, sent)
+    own_copy(0).start()
     pl.semaphore_wait(barrier, n)
-
-    each(1, n, lambda k: x_copy(k).start())
-    each(1, n, lambda k: g_copy(k).start())
+    each(0, n, later(x_copy))
+    mixed[...] = (prob[...] * cotangent[...].astype(jnp.float32)).astype(jnp.bfloat16)
+    dispatch(mixed, sent_grad)
+    own_copy(1).start()
+    each(0, n, later(g_copy))
     own_copy(0).wait()
     own_copy(1).wait()
     weight_copy(0).wait()
     weight_copy(1).wait()
 
+    def span(first):
+        return pl.ds(pl.multiple_of(first * cap, rows), rows)
+
     def forward(g):
-        first = g * group
+        first = lax.rem((1 - core) * (g + groups // 4) + core * (groups // 4 * 3 - 1 - g + groups), groups) * group
 
         def arrived(k):
             @pl.when(k > 0)
@@ -135,7 +169,7 @@
             value = value.reshape(group, cap, tile) * scale
             slope = slope.reshape(group, cap, tile) * scale
             hidden[pl.ds(first, group), :, columns] = value.astype(jnp.bfloat16)
-            factor[pl.ds(first, group), :, columns] = slope
+            factor[span(first), columns] = slope.reshape(rows, tile)
 
         each(0, ff // tile, project)
 
@@ -161,7 +195,7 @@
     each(0, groups, forward)
 
     def backward(g):
-        first = g * group
+        first = lax.rem((1 - core) * (g + groups // 4) + core * (groups // 4 * 3 - 1 - g + groups), groups) * group
 
         def arrived(k):
             @pl.when(k > 0)
@@ -177,8 +211,8 @@
                 block, weight_out[columns, :], (((1,), (1,)), ((), ())),
                 preferred_element_type=jnp.float32,
             )
-            dhidden = dhidden.reshape(group, cap, tile) * factor[pl.ds(first, group), :, columns]
-            dpre[pl.ds(first, group), :, columns] = dhidden.astype(jnp.bfloat16)
+            dhidden = (dhidden * factor[span(first), columns]).astype(jnp.bfloat16)
+            dpre[pl.ds(first, group), :, columns] = dhidden.reshape(group, cap, tile)
 
         each(0, ff // tile, pull)
 
@@ -193,7 +227,7 @@
 
     def gradient(i, left, right, give, came):
         half = give.shape[0]
-        part = tile_of(half, 128)
+        part = tile_of(half, 256)
 
         def theirs(j):
             give[pl.ds(pl.multiple_of(j * part, part), part), :] = product(
@@ -224,8 +258,19 @@
         x_copy(k).wait_send()
         g_copy(k).wait_send()
         o_copy(k).wait_send()
-        o_copy(k).wait_recv()
-
+
+    each(1, n, lambda k: o_copy(k).wait_recv())
+
+    def combine(j):
+        columns = pl.ds(pl.multiple_of(j * wide, wide), wide)
+        place = lax.broadcasted_iota(jnp.int32, (count, n * cap), 1)
+        chosen = jnp.where(place == slot_column[...], 1.0, 0.0).astype(jnp.bfloat16)
+        out = jnp.dot(
+            chosen, back[:, :, columns].reshape(n * cap, wide), preferred_element_type=jnp.float32
+        )
+        mixed[:, columns] = (prob[...] * out).astype(jnp.bfloat16)
+
+    each(0, width // wide, combine)
     each(1, n, finish)
     pair_copy(0).wait_send()
     pair_copy(1).wait_send()
@@ -233,8 +278,8 @@
     result_copy(1).wait()
 
 
-def exchange(sent, sent_grad, keep, w_in, w_out):
-    n, cap, width = sent.shape
+def exchange(n, cap, tokens, cotangent, prob, target, keep, w_in, w_out):
+    count, width = tokens.shape
     ff = w_in.shape[1]
     group = min(n, max(1, 256 // cap))
     dma = pltpu.SemaphoreType.DMA
@@ -244,33 +289,35 @@
     return pl.pallas_call(
         functools.partial(kernel, n, group),
         out_shape=(
-            jax.ShapeDtypeStruct((n, cap, width), bf16),
+            jax.ShapeDtypeStruct((count, width), bf16),
             jax.ShapeDtypeStruct((width // 2, ff), f32),
             jax.ShapeDtypeStruct((ff // 2, width), f32),
         ),
-        in_specs=[whole, whole, pl.BlockSpec(memory_space=pltpu.VMEM), whole, whole],
-        out_specs=(whole, whole, whole),
+        in_specs=[pl.BlockSpec(memory_space=pltpu.VMEM)] * 6 + [whole, whole],
+        out_specs=(pl.BlockSpec(memory_space=pltpu.VMEM), whole, whole),
         scratch_shapes=[
+            pltpu.VMEM((n, cap, width), bf16),
+            pltpu.VMEM((n, cap, width), bf16),
+            pltpu.VMEM((n, cap, width), bf16),
             pltpu.VMEM((width, ff), bf16),
             pltpu.VMEM((ff, width), bf16),
             pltpu.VMEM((n, cap, width), bf16),
             pltpu.VMEM((n, cap, width), bf16),
             pltpu.VMEM((n, cap, width), bf16),
             pltpu.VMEM((n, cap, ff), bf16),
-            pltpu.VMEM((n, cap, ff), f32),
+            pltpu.VMEM((n * cap, ff), f32),
             pltpu.VMEM((n, cap, ff), bf16),
             pltpu.VMEM((ff // 2, width), f32),
             pltpu.VMEM((ff // 2, width), f32),
-            pltpu.VMEM((width // 2, ff), f32),
             pltpu.VMEM((width // 2, ff), f32),
             dma((2,)), dma((3,)), dma((n,)), dma((n,)), dma((n,)), dma((n,)), dma((n,)), dma((n,)),
             dma((2,)), dma((2,)), dma((2,)),
         ],
         cost_estimate=pl.CostEstimate(flops=flops, bytes_accessed=40 << 20, transcendentals=n * cap * ff),
         compiler_params=pltpu.CompilerParams(
-            collective_id=0, has_side_effects=True, vmem_limit_bytes=60 << 20
+            collective_id=0, has_side_effects=True, vmem_limit_bytes=67043328
         ),
-    )(sent, sent_grad, keep, w_in, w_out)
+    )(tokens, cotangent, prob[:, None], target[None, :], target[:, None], keep, w_in, w_out)
 
 
 def shards(tokens, expert_id, router_prob, keep_mask, w_in, w_out, cotangent):
@@ -285,13 +332,6 @@
     onehot = (ids[:, None] == jnp.arange(n_expert, dtype=jnp.int32)[None, :]).astype(jnp.int32)
     ranks = jnp.sum(jnp.cumsum(onehot, axis=0) * onehot, axis=1) - 1
     target = ids * capacity + ranks % n_replica * portion + ranks // n_replica
-
-    def fill_slots(values):
-        return jnp.zeros((n_expert * capacity, width), values.dtype).at[target].set(values)
-
-    sent = fill_slots(tokens)
-    gated = (router_prob[:, None] * cotangent.astype(jnp.float32)).astype(jnp.bfloat16)
-    sent_grad = fill_slots(gated)
     keep_rows = lax.dynamic_index_in_dim(
         keep_mask[0].reshape(n_expert, n_replica, -1),
         lax.axis_index("replica"),
@@ -301,15 +341,9 @@
     keep_scale = keep_rows.astype(jnp.float32) * KEEP_SCALE
     sources = (lax.axis_index("expert") - jnp.arange(n_expert) + n_expert) % n_expert
     keep_scale = keep_scale[sources][:, None, :]
-    returned, grad_in, grad_out = exchange(
-        sent.reshape(n_expert, capacity, width),
-        sent_grad.reshape(n_expert, capacity, width),
-        keep_scale,
-        weight_in,
-        weight_out,
-    )
-    expert_out = returned.reshape(n_expert * capacity, width)[target]
-    mixed = (router_prob[:, None] * expert_out.astype(jnp.float32)).astype(jnp.bfloat16)
+    mixed, grad_in, grad_out = exchange(
+        n_expert, capacity, tokens, cotangent, router_prob, target, keep_scale, weight_in, weight_out
+    )
     return (mixed, grad_in[None], grad_out[None])
 
 

time: 180 us -> 170 us (0.944)
  local copies, waits for them, and re-layouts: 19.1 us -> 14.4 us
  Pallas kernels: 153 us -> 150 us
  other arithmetic: 6.8 us -> 4.31 us
    scatter x1 -> x0, local copies, waits for them, and re-layouts: 4.79 us -> none  [fill_slots(): jnp.zeros((n_expert * capacity, width), values.dtype).at[target].set(values)]
    gather x1 -> x0, local copies, waits for them, and re-layouts: 4.59 us -> none  [shards(): expert_out = returned.reshape(n_expert * capacity, width)[target]]
    scatter x1 -> x0, other arithmetic: 4.19 us -> none  [fill_slots(): jnp.zeros((n_expert * capacity, width), values.dtype).at[target].set(values)]
    unnamed x10 -> x6, local copies, waits for them, and re-layouts: 6.88 us -> 9.95 us
    pallas_call x1, Pallas kernels: 153 us -> 150 us  [exchange(): pl.pallas_call(functools.partial(kernel, n, group), out_shape=(jax.ShapeD...]
where the time goes in v3:
time: 170 us
  Pallas kernels  150 us (88%)
  local copies, waits for them, and re-layouts  14.4 us (8%)
  other arithmetic  4.31 us (3%)
    pallas_call x1, Pallas kernels, exchange(): pl.pallas_call(functools.partial(kernel, n, group), out_shape=(jax.ShapeD...  150 us
    unnamed x6, local copies, waits for them, and re-layouts  9.95 us

profile of v3, /device:TPU:0, one launch (start us, length us, event | category | flops | bytes accessed | tf_op | source)
XLA Modules:
  0.0 169.7 jit_solution(8668759913019401630)
XLA Ops:
  0.7 0.7 fusion.11
  1.4 1.1 reduce-window.6
  2.5 0.2 slice_reduce_fusion
  2.7 0.8 fusion.10
  3.5 0.1 copy.13
  3.7 1.5 copy.18.prob
  5.2 1.1 reshape_squeeze.3
  6.3 0.1 constant_dynamic-slice_fusion
  6.5 0.1 fusion.8
  6.5 0.6 gather_fusion
  7.1 0.7 broadcast_in_dim.17.keep
  7.9 0.8 copy.11
  8.7 1.0 fusion.2
  9.7 0.6 fusion.14.slot_row
  10.3 150.2 %shard_map.94 = (bf16[512,1024]{1,0:T(8,128)(2,1)}, f32[512,2048]{1,0:T(8,128)}, f32[1024,1024]{1,0:T(8,128)}) custom-call(bf16[512,1024]{1,0:T(8,128)(2,1)} %tokens.1, bf16[512,1024]{1,0:T(8,128)(2,1)} %cotangent.1, f32[512,1]{1,0:T(8,128)} %copy.18.prob, s32[1,512]{1,0:T(1,128)} %fusion.14.slot_row, s32[512,1]{1,0:T(8,128)} %get-tuple-element.9.slot_column, ...), custom_call_target="tpu_custom_call" | custom-call | flops 21474836480 | bytes 41943040 | tf_op jit(solution)/shard_map/pallas_call | solution.py:289
  160.5 2.3 %copy.30 = bf16[512,1024]{1,0:T(8,128)(2,1)} copy(bf16[512,1024]{1,0:T(8,128)(2,1)} %get-tuple-element.14) | data formatting | bytes 2097152
  162.8 0.0 copy-start
  162.8 4.8 %copy.31 = f32[1,512,2048]{2,1,0:T(8,128)} copy(f32[1,512,2048]{2,1,0:T(8,128)} %bitcast.30) | data formatting | bytes 8388608
  167.6 0.0 copy-done
  167.6 2.0 %copy.32 = f32[1,1024,1024]{2,1,0:T(8,128)} copy(f32[1,1024,1024]{2,1,0:T(8,128)S(1)} %bitcast.29) | data formatting | bytes 8388608
  (5 shorter events, 0.1 us)
Async XLA Ops:
  162.8 4.9 %copy-start = (f32[1024,1024]{1,0:T(8,128)S(1)}, f32[1024,1024]{1,0:T(8,128)}, u32[]{:S(2)}) copy-start(f32[1024,1024]{1,0:T(8,128)} %get-tuple-element.8) | copy-start | bytes 12582916
